TPU v7x, 32 devices: a whole 2x2x4 slice. The times are simulated.
32 devices in a mesh: part: 2 (over x), data: 4 (over z), model: 4 (over y, core).
Axes of the slice: x: 2, y: 2, z: 4, core: 2. Of those that a mesh axis runs over, the one named last changes fastest.
Arguments:
- x: bfloat16 [2, 8, 2048, 2048], P(None, ('part', 'data'), 'model'), parts along dimension 1
- lengths: int32 [2, 8], P(None, ('part', 'data')), parts along dimension 1
- norm_gain: bfloat16 [2, 2048], P(None, 'data')
- w_in: bfloat16 [2, 2048, 18432], P(None, 'data', 'model')
- w_kv: bfloat16 [2, 2048, 512], P(None, 'data')
- w_out: bfloat16 [2, 10240, 2048], P(None, 'model', 'data')
Outputs:
- output: bfloat16 [2, 8, 2048, 2048], P(None, ('part', 'data'), 'model'), parts along dimension 1
There are 2 independent parts. A program takes and returns all parts, laid end to end along the dimension named above; an argument that names none is the same for every part.
All inputs are finite; a program needn't handle non-finite values.
Results may differ from a plain program's by a relative error of at most 0.0147284.
Values are sent between devices in bfloat16 or wider.
A program may use at most 1 GiB of HBM per device.

v0:
```python
import math
import jax
import jax.numpy as jnp
from jax import lax
from jax.sharding import PartitionSpec as P, NamedSharding

NORM_EPS = 1e-6
NEG_BIG = -1e30


def layer_norm(x_act, gain_vec):
    x_f32 = x_act.astype(jnp.float32)
    centered = x_f32 - jnp.mean(x_f32, axis=-1, keepdims=True)
    variance = jnp.mean(centered * centered, axis=-1, keepdims=True)
    return (centered * lax.rsqrt(variance + NORM_EPS) * gain_vec.astype(jnp.float32)).astype(jnp.bfloat16)


def attention(q_heads, k_all, v_all, seq_lens, q_offset):
    q_len = q_heads.shape[1]
    k_len = k_all.shape[1]
    head_dim = k_all.shape[2]
    scores = jnp.einsum("bqhc,bkc->bhqk", q_heads, k_all, preferred_element_type=jnp.float32) * (1.0 / math.sqrt(head_dim))
    q_pos = q_offset + lax.broadcasted_iota(jnp.int32, (q_len, 1), 0)
    k_pos = lax.broadcasted_iota(jnp.int32, (1, k_len), 1)
    allowed = (k_pos <= q_pos)[None, None] & (k_pos[None, None] < seq_lens[:, None, None, None])
    scores = jnp.where(allowed, scores, NEG_BIG)
    attn_probs = jax.nn.softmax(scores, axis=-1).astype(jnp.bfloat16)
    return jnp.einsum("bhqk,bkc->bqhc", attn_probs, v_all, preferred_element_type=jnp.float32).astype(jnp.bfloat16)


def layer_block(x_loc, seq_lens, gain_full, w_in3, w_kv_full, w_out3, n_model):
    n_seqs, t_loc, d_model = x_loc.shape
    head_dim = w_kv_full.shape[1] // 2
    ff_head = (w_in3.shape[2] - head_dim) // 2
    h_loc = layer_norm(x_loc, gain_full)
    h_all = lax.all_gather(h_loc, "model", axis=1, tiled=True)
    projected = jnp.einsum("btd,dhc->bthc", h_all, w_in3, preferred_element_type=jnp.float32).astype(jnp.bfloat16)
    kv_act = jnp.einsum("btd,dc->btc", h_all, w_kv_full, preferred_element_type=jnp.float32).astype(jnp.bfloat16)
    attn_out = attention(projected[..., :head_dim], kv_act[..., :head_dim], kv_act[..., head_dim:], seq_lens, 0)
    gate_act = projected[..., head_dim:head_dim + ff_head]
    up_act = projected[..., head_dim + ff_head:]
    mlp_out = (jax.nn.silu(gate_act.astype(jnp.float32)) * up_act.astype(jnp.float32)).astype(jnp.bfloat16)
    joined = jnp.concatenate([attn_out, mlp_out], axis=-1)
    group_sum = jnp.einsum("bthc,hcd->btd", joined, w_out3, preferred_element_type=jnp.float32).astype(jnp.bfloat16)
    received = lax.all_to_all(group_sum.reshape(n_seqs, n_model, t_loc, d_model), "model", 1, 1, tiled=True)
    z_sum = jnp.sum(received.astype(jnp.float32), axis=1)
    return (x_loc.astype(jnp.float32) + z_sum).astype(jnp.bfloat16)


def solution(mesh):
    n_model = mesh.shape["model"]
    act_spec = P(None, ("part", "data"), "model", None)

    def local_fn(x_blk, len_blk, gain_blk, w_in_blk, w_kv_blk, w_out_blk):
        head_dim = w_kv_blk.shape[2] // 2
        hidden = [x_blk[micro_idx] for micro_idx in range(x_blk.shape[0])]
        for layer_idx in range(gain_blk.shape[0]):
            gain_full = lax.all_gather(gain_blk[layer_idx], "data", axis=0, tiled=True)
            w_in_loc = lax.all_gather(w_in_blk[layer_idx], "data", axis=0, tiled=True)
            w_kv_full = lax.all_gather(w_kv_blk[layer_idx], "data", axis=0, tiled=True)
            w_out_loc = lax.all_gather(w_out_blk[layer_idx], "data", axis=1, tiled=True)
            d_model, in_loc = w_in_loc.shape
            out_loc = w_out_loc.shape[0]
            ff_loc = in_loc - out_loc
            heads_loc = (out_loc - ff_loc) // head_dim
            w_in3 = w_in_loc.reshape(d_model, heads_loc, in_loc // heads_loc)
            w_out3 = w_out_loc.reshape(heads_loc, out_loc // heads_loc, d_model)
            for micro_idx in range(len(hidden)):
                hidden[micro_idx] = layer_block(hidden[micro_idx], len_blk[micro_idx], gain_full, w_in3, w_kv_full, w_out3, n_model)
        return jnp.stack(hidden)

    return jax.shard_map(
        local_fn,
        mesh=mesh,
        in_specs=(act_spec, P(None, ("part", "data")), P(None, "data"), P(None, "data", "model"), P(None, "data", None), P(None, "model", "data")),
        out_specs=act_spec,
        check_vma=False,
    )
```

profile of v0, /device:TPU:8, one launch (start us, length us, event | category | flops | bytes accessed | tf_op | source)
XLA Modules:
  0.0 1634.7 jit_solution(13608933335736108663)
XLA Ops:
  72.4 42.3 %all-gather.23.cloned.1.call-done = bf16[1,2048,2048]{2,1,0:T(8,128)(2,1)} async-done(((bf16[1,512,2048]{2,1,0:T(8,128)(2,1)}), bf16[1,2048,2048]{2,1,0:T(8,128)(2,1)}) %all-gather.23.cloned.1.call-update) | async-done | bytes 8388624 | tf_op jit(solution)/shard_map/all_gather | solution.py:36
  124.5 50.3 %all-gather.19.cloned.1.call-done = bf16[1,2048,2048]{2,1,0:T(8,128)(2,1)} async-done(((bf16[1,512,2048]{2,1,0:T(8,128)(2,1)}), bf16[1,2048,2048]{2,1,0:T(8,128)(2,1)}) %all-gather.19.cloned.1.call-update) | async-done | bytes 8388624 | tf_op jit(solution)/shard_map/all_gather | solution.py:36
  183.9 313.5 %all-gather.29.cloned.1.call-done = bf16[1,2048,4608]{1,2,0:T(8,128)(2,1)} async-done(((bf16[1,512,4608]{1,2,0:T(8,128)(2,1)}), bf16[1,2048,4608]{1,2,0:T(8,128)(2,1)}) %all-gather.29.cloned.1.call-update) | async-done | bytes 18874384 | tf_op jit(solution)/shard_map/all_gather | solution.py:59
  497.4 45.4 %convert_bitcast_fusion.1 = bf16[1,2048,2,2304]{3,1,2,0:T(8,128)(2,1)S(1)} fusion(bf16[2048,2,2304]{0,2,1:T(8,128)(2,1)} %bitcast.394, bf16[1,2048,2048]{2,1,0:T(8,128)(2,1)} %all-gather.23.cloned.1.call-done), kind=kOutput, calls=%fused_computation.29 | convolution fusion | flops 38664142848 | bytes 46137344 | tf_op jit(solution)/shard_map/btd,dhc->bthc/dot_general | solution.py:37
  586.4 17.0 %fusion.113 = bf16[1,2048,2,256]{3,1,2,0:T(8,128)(2,1)} fusion(f32[2,2048]{1,0:T(2,128)S(1)} %fusion.2, f32[2,2048]{1,0:T(2,128)S(1)} %get-tuple-element.31, f32[2048,2048,2]{1,0,2:T(8,128)} %get-tuple-element.32, pred[2048,2048]{0,1:T(8,128)(4,1)S(1)} %copy-done.9, bf16[1,2048,512]{2,1,0:T(8,128)(2,1)S(1)} %copy-done.18), kind=kOutput, calls=%fused_computation.151 | convolution fusion | flops 4337958912 | bytes 40927232 | tf_op jit(solution)/shard_map/bhqk,bkc->bqhc/dot_general | solution.py:28
  603.4 77.7 %all-gather.31.cloned.1.call-done = bf16[1,2560,2048]{2,1,0:T(8,128)(2,1)} async-done(((bf16[1,2560,512]{2,1,0:T(8,128)(2,1)}), bf16[1,2560,2048]{2,1,0:T(8,128)(2,1)}) %all-gather.31.cloned.1.call-update) | async-done | bytes 10485776 | tf_op jit(solution)/shard_map/all_gather | solution.py:61
  681.1 28.5 %bitcast_convert_fusion.1 = bf16[2048,2048]{1,0:T(8,128)(2,1)} fusion(bf16[2,1280,2048]{2,1,0:T(8,128)(2,1)} %bitcast.396, bf16[1,2048,2,1024]{3,1,2,0:T(8,128)(2,1)} %fusion.35, bf16[1,2048,2,256]{3,1,2,0:T(8,128)(2,1)} %fusion.113), kind=kOutput, calls=%fused_computation.51 | convolution fusion | flops 21500002304 | bytes 29360128 | tf_op jit(solution)/shard_map/bthc,hcd->btd/dot_general | solution.py:44
  715.5 47.0 %convert_bitcast_fusion.3 = bf16[1,2048,2,2304]{3,1,2,0:T(8,128)(2,1)} fusion(bf16[2048,2,2304]{0,2,1:T(8,128)(2,1)} %bitcast.395, bf16[1,2048,2048]{2,1,0:T(8,128)(2,1)} %all-gather.19.cloned.1.call-done), kind=kOutput, calls=%fused_computation.31 | convolution fusion | flops 38664142848 | bytes 46137344 | tf_op jit(solution)/shard_map/btd,dhc->bthc/dot_general | solution.py:37
  778.0 16.6 %fusion = f32[2,2048]{1,0:T(2,128)S(1)} fusion(f32[2048,2048,2]{1,0,2:T(8,128)} %get-tuple-element.30, f32[2,2048]{1,0:T(2,128)S(1)} %get-tuple-element.29, pred[2048,2048]{0,1:T(8,128)(4,1)} %fusion.33), kind=kLoop, calls=%fused_computation.12 | loop fusion | flops 33550336 | bytes 37781504 | tf_op jit(solution)/shard_map/reduce_sum | solution.py:27
  819.7 24.1 %bitcast_convert_fusion.3 = bf16[2048,2048]{1,0:T(8,128)(2,1)} fusion(bf16[2,1280,2048]{2,1,0:T(8,128)(2,1)S(1)} %bitcast.399, bf16[1,2048,2,1024]{3,1,2,0:T(8,128)(2,1)S(1)} %fusion.37, bf16[1,2048,2,256]{3,1,2,0:T(8,128)(2,1)S(1)} %fusion.119), kind=kOutput, calls=%fused_computation.57 | convolution fusion | flops 21500002304 | bytes 29360128 | tf_op jit(solution)/shard_map/bthc,hcd->btd/dot_general | solution.py:44
  849.7 18.6 %all-gather.4 = bf16[1,2048]{1,0:T(2,128)(2,1)S(1)} all-gather(bf16[1,512]{1,0:T(2,128)(2,1)S(1)} %copy-done.12), channel_id=6, replica_groups=mesh['part'=2,'data'=4,'model'=4] {'data'}, dimensions={1}, use_global_device_ids=true | all-gather | bytes 5120 | tf_op jit(solution)/shard_map/all_gather | solution.py:58
  876.0 66.5 %all-to-all-done = bf16[1,4,512,2048]{3,2,0,1:T(8,128)(2,1)} async-done(((bf16[1,4,512,2048]{3,2,0,1:T(8,128)(2,1)}), bf16[1,4,512,2048]{3,2,0,1:T(8,128)(2,1)}, u32[]{:S(2)}, u32[]{:S(2)}) %all-to-all-start) | async-done | bytes 8388640 | tf_op jit(solution)/shard_map/all_to_all | solution.py:45
  956.3 49.7 %all-gather.35.cloned.1.call-done = bf16[1,2048,4608]{1,2,0:T(8,128)(2,1)} async-done(((bf16[1,512,4608]{1,2,0:T(8,128)(2,1)}), bf16[1,2048,4608]{1,2,0:T(8,128)(2,1)}) %all-gather.35.cloned.1.call-update) | async-done | bytes 18874384 | tf_op jit(solution)/shard_map/all_gather | solution.py:59
  1006.0 61.2 %all-gather.25.cloned.1.call-done = bf16[1,2048,2048]{2,1,0:T(8,128)(2,1)} async-done(((bf16[1,512,2048]{2,1,0:T(8,128)(2,1)}), bf16[1,2048,2048]{2,1,0:T(8,128)(2,1)}) %all-gather.25.cloned.1.call-update) | async-done | bytes 8388624 | tf_op jit(solution)/shard_map/all_gather | solution.py:36
  1067.2 47.0 %convert_bitcast_fusion = bf16[1,2048,2,2304]{3,1,2,0:T(8,128)(2,1)} fusion(bf16[2048,2,2304]{0,2,1:T(8,128)(2,1)} %bitcast.392, bf16[1,2048,2048]{2,1,0:T(8,128)(2,1)} %all-gather.25.cloned.1.call-done), kind=kOutput, calls=%fused_computation.28 | convolution fusion | flops 38664142848 | bytes 46137344 | tf_op jit(solution)/shard_map/btd,dhc->bthc/dot_general | solution.py:37
  1165.1 16.8 %fusion.110 = bf16[1,2048,2,256]{3,1,2,0:T(8,128)(2,1)} fusion(f32[2,2048]{1,0:T(2,128)S(1)} %fusion.3, f32[2,2048]{1,0:T(2,128)S(1)} %get-tuple-element.35, f32[2048,2048,2]{1,0,2:T(8,128)} %get-tuple-element.36, pred[2048,2048]{0,1:T(8,128)(4,1)S(1)} %copy-done.10, bf16[1,2048,512]{2,1,0:T(8,128)(2,1)S(1)} %fusion.122), kind=kOutput, calls=%fused_computation.150 | convolution fusion | flops 4337958912 | bytes 40927232 | tf_op jit(solution)/shard_map/bhqk,bkc->bqhc/dot_general | solution.py:28
  1181.9 113.9 %all-gather.37.cloned.1.call-done = bf16[1,2560,2048]{2,1,0:T(8,128)(2,1)} async-done(((bf16[1,2560,512]{2,1,0:T(8,128)(2,1)}), bf16[1,2560,2048]{2,1,0:T(8,128)(2,1)}) %all-gather.37.cloned.1.call-update) | async-done | bytes 10485776 | tf_op jit(solution)/shard_map/all_gather | solution.py:61
  1295.8 28.4 %bitcast_convert_fusion = bf16[2048,2048]{1,0:T(8,128)(2,1)} fusion(bf16[2,1280,2048]{2,1,0:T(8,128)(2,1)} %bitcast.400, bf16[1,2048,2,1024]{3,1,2,0:T(8,128)(2,1)} %fusion.34, bf16[1,2048,2,256]{3,1,2,0:T(8,128)(2,1)} %fusion.110), kind=kOutput, calls=%fused_computation.48 | convolution fusion | flops 21500002304 | bytes 29360128 | tf_op jit(solution)/shard_map/bthc,hcd->btd/dot_general | solution.py:44
  1330.1 49.6 %all-gather.21.cloned.1.call-done = bf16[1,2048,2048]{2,1,0:T(8,128)(2,1)} async-done(((bf16[1,512,2048]{2,1,0:T(8,128)(2,1)}), bf16[1,2048,2048]{2,1,0:T(8,128)(2,1)}) %all-gather.21.cloned.1.call-update) | async-done | bytes 8388624 | tf_op jit(solution)/shard_map/all_gather | solution.py:36
  1379.7 47.6 %convert_bitcast_fusion.2 = bf16[1,2048,2,2304]{3,1,2,0:T(8,128)(2,1)} fusion(bf16[2048,2,2304]{0,2,1:T(8,128)(2,1)} %bitcast.393, bf16[1,2048,2048]{2,1,0:T(8,128)(2,1)} %all-gather.21.cloned.1.call-done), kind=kOutput, calls=%fused_computation.30 | convolution fusion | flops 38664142848 | bytes 46137344 | tf_op jit(solution)/shard_map/btd,dhc->bthc/dot_general | solution.py:37
  1433.1 16.4 %fusion.5 = (f32[2,2048]{1,0:T(2,128)S(1)}, f32[2048,2048,2]{1,0,2:T(8,128)}) fusion(pred[2048,2048]{0,1:T(8,128)(4,1)} %fusion.33, bf16[1,2048,2,2304]{3,1,2,0:T(8,128)(2,1)} %convert_bitcast_fusion.2, bf16[1,2048,512]{2,1,0:T(8,128)(2,1)} %fusion.128), kind=kOutput, calls=%fused_computation.17 | convolution fusion | flops 4320129024 | bytes 40910848 | tf_op jit(solution)/shard_map/bqhc,bkc->bhqk/dot_general | solution.py:22
  1449.5 16.7 %fusion.1 = f32[2,2048]{1,0:T(2,128)S(1)} fusion(f32[2048,2048,2]{1,0,2:T(8,128)} %get-tuple-element.34, f32[2,2048]{1,0:T(2,128)S(1)} %get-tuple-element.33, pred[2048,2048]{0,1:T(8,128)(4,1)} %fusion.33), kind=kLoop, calls=%fused_computation.13 | loop fusion | flops 33550336 | bytes 37781504 | tf_op jit(solution)/shard_map/reduce_sum | solution.py:27
  1490.9 24.1 %bitcast_convert_fusion.2 = bf16[2048,2048]{1,0:T(8,128)(2,1)} fusion(bf16[2,1280,2048]{2,1,0:T(8,128)(2,1)S(1)} %bitcast.403, bf16[1,2048,2,1024]{3,1,2,0:T(8,128)(2,1)S(1)} %fusion.36, bf16[1,2048,2,256]{3,1,2,0:T(8,128)(2,1)S(1)} %fusion.116), kind=kOutput, calls=%fused_computation.54 | convolution fusion | flops 21500002304 | bytes 29360128 | tf_op jit(solution)/shard_map/bthc,hcd->btd/dot_general | solution.py:44
  1528.6 85.1 %all-to-all-done.1 = bf16[1,4,512,2048]{3,2,0,1:T(8,128)(2,1)} async-done(((bf16[1,4,512,2048]{3,2,0,1:T(8,128)(2,1)}), bf16[1,4,512,2048]{3,2,0,1:T(8,128)(2,1)}, u32[]{:S(2)}, u32[]{:S(2)}) %all-to-all-start.1) | async-done | bytes 8388640 | tf_op jit(solution)/shard_map/all_to_all | solution.py:45
  (130 shorter events, 316.2 us)
Async XLA Ops:
  6.5 65.9 %all-gather.27.cloned.1.call-start = ((), (), s32[]{:S(2)}) async-start(), calls=%async_computation.8 | async-start | bytes 2621440 | tf_op jit(solution)/shard_map/all_gather | solution.py:60
  8.8 105.8 %all-gather.23.cloned.1.call-start = ((), (), s32[]{:S(2)}) async-start(), calls=%async_computation.6 | async-start | bytes 10485760 | tf_op jit(solution)/shard_map/all_gather | solution.py:36
  32.4 142.4 %all-gather.19.cloned.1.call-start = ((), (), s32[]{:S(2)}) async-start(), calls=%async_computation.4 | async-start | bytes 10485760 | tf_op jit(solution)/shard_map/all_gather | solution.py:36
  33.2 464.2 %all-gather.29.cloned.1.call-start = ((), (), s32[]{:S(2)}) async-start(), calls=%async_computation.9 | async-start | bytes 23592960 | tf_op jit(solution)/shard_map/all_gather | solution.py:59
  47.9 633.2 %all-gather.31.cloned.1.call-start = ((), (), s32[]{:S(2)}) async-start(), calls=%async_computation.10 | async-start | bytes 13107200 | tf_op jit(solution)/shard_map/all_gather | solution.py:61
  53.1 952.9 %all-gather.35.cloned.1.call-start = ((), (), s32[]{:S(2)}) async-start(), calls=%async_computation.12 | async-start | bytes 23592960 | tf_op jit(solution)/shard_map/all_gather | solution.py:59
  72.4 102.4 %copy-start.15 = (bf16[1,2048,512]{2,1,0:T(8,128)(2,1)S(1)}, bf16[1,2048,512]{2,1,0:T(8,128)(2,1)}, u32[]{:S(2)}) copy-start(bf16[1,2048,512]{2,1,0:T(8,128)(2,1)} %all-gather.27.cloned.1.call-done) | copy-start | bytes 6291460
  709.6 134.3 %all-to-all-start.2 = ((bf16[1,4,512,2048]{3,2,0,1:T(8,128)(2,1)}), bf16[1,4,512,2048]{3,2,0,1:T(8,128)(2,1)}, u32[]{:S(2)}, u32[]{:S(2)}) async-start(bf16[1,4,512,2048]{3,2,0,1:T(8,128)(2,1)} %bitcast.387), calls=%async_computation.2 | async-start | bytes 16777216 | tf_op jit(solution)/shard_map/all_to_all | solution.py:45
  715.5 47.1 %copy-start.17 = (bf16[1,2048,512]{2,1,0:T(8,128)(2,1)S(1)}, bf16[1,2048,512]{2,1,0:T(8,128)(2,1)}, u32[]{:S(2)}) copy-start(bf16[1,2048,512]{2,1,0:T(8,128)(2,1)} %fusion.131) | copy-start | bytes 6291460
  778.0 41.7 %slice-start = ((s8[10485760]{0:T(1024)(128)(4,1)}), s8[4194304]{0:T(1024)(128)(4,1)S(1)}, s32[]{:S(2)}) async-start(s8[10485760]{0:T(1024)(128)(4,1)} %bitcast.397), calls=%async_computation.14 | async-start | bytes 8388608
  794.6 25.1 %slice-start.1 = ((s8[10485760]{0:T(1024)(128)(4,1)}), s8[4194304]{0:T(1024)(128)(4,1)S(1)}, s32[]{:S(2)}) async-start(s8[10485760]{0:T(1024)(128)(4,1)} %bitcast.397), calls=%async_computation.15 | async-start | bytes 8388608
  794.6 25.1 %slice-start.2 = ((s8[10485760]{0:T(1024)(128)(4,1)}), s8[2097152]{0:T(1024)(128)(4,1)S(1)}, s32[]{:S(2)}) async-start(s8[10485760]{0:T(1024)(128)(4,1)} %bitcast.397), calls=%async_computation.16 | async-start | bytes 4194304
  843.8 98.7 %all-to-all-start = ((bf16[1,4,512,2048]{3,2,0,1:T(8,128)(2,1)}), bf16[1,4,512,2048]{3,2,0,1:T(8,128)(2,1)}, u32[]{:S(2)}, u32[]{:S(2)}) async-start(bf16[1,4,512,2048]{3,2,0,1:T(8,128)(2,1)} %bitcast.388), calls=%async_computation | async-start | bytes 16777216 | tf_op jit(solution)/shard_map/all_to_all | solution.py:45
  849.7 217.5 %all-gather.25.cloned.1.call-start = ((), (), s32[]{:S(2)}) async-start(), calls=%async_computation.7 | async-start | bytes 10485760 | tf_op jit(solution)/shard_map/all_gather | solution.py:36
  954.2 160.0 %all-gather.33.cloned.1.call-start = ((), (), s32[]{:S(2)}) async-start(), calls=%async_computation.11 | async-start | bytes 2621440 | tf_op jit(solution)/shard_map/all_gather | solution.py:60
  955.0 340.9 %all-gather.37.cloned.1.call-start = ((), (), s32[]{:S(2)}) async-start(), calls=%async_computation.13 | async-start | bytes 13107200 | tf_op jit(solution)/shard_map/all_gather | solution.py:61
  955.7 424.0 %all-gather.21.cloned.1.call-start = ((), (), s32[]{:S(2)}) async-start(), calls=%async_computation.5 | async-start | bytes 10485760 | tf_op jit(solution)/shard_map/all_gather | solution.py:36
  1324.3 190.7 %all-to-all-start.3 = ((bf16[1,4,512,2048]{3,2,0,1:T(8,128)(2,1)}), bf16[1,4,512,2048]{3,2,0,1:T(8,128)(2,1)}, u32[]{:S(2)}, u32[]{:S(2)}) async-start(bf16[1,4,512,2048]{3,2,0,1:T(8,128)(2,1)} %bitcast.386), calls=%async_computation.3 | async-start | bytes 16777216 | tf_op jit(solution)/shard_map/all_to_all | solution.py:45
  1330.1 97.3 %copy-start.16 = (bf16[1,2048,512]{2,1,0:T(8,128)(2,1)S(1)}, bf16[1,2048,512]{2,1,0:T(8,128)(2,1)}, u32[]{:S(2)}) copy-start(bf16[1,2048,512]{2,1,0:T(8,128)(2,1)} %all-gather.33.cloned.1.call-done) | copy-start | bytes 6291460
  1379.7 47.6 %copy-start.14 = (bf16[1,2048,2048]{2,1,0:T(8,128)(2,1)S(1)}, bf16[1,2048,2048]{2,1,0:T(8,128)(2,1)}, u32[]{:S(2)}) copy-start(bf16[1,2048,2048]{2,1,0:T(8,128)(2,1)} %all-gather.21.cloned.1.call-done) | copy-start | bytes 25165828
  1449.5 41.3 %slice-start.3 = ((s8[10485760]{0:T(1024)(128)(4,1)}), s8[4194304]{0:T(1024)(128)(4,1)S(1)}, s32[]{:S(2)}) async-start(s8[10485760]{0:T(1024)(128)(4,1)} %bitcast.401), calls=%async_computation.17 | async-start | bytes 8388608
  1466.3 24.6 %slice-start.4 = ((s8[10485760]{0:T(1024)(128)(4,1)}), s8[4194304]{0:T(1024)(128)(4,1)S(1)}, s32[]{:S(2)}) async-start(s8[10485760]{0:T(1024)(128)(4,1)} %bitcast.401), calls=%async_computation.18 | async-start | bytes 8388608
  1466.3 24.6 %slice-start.5 = ((s8[10485760]{0:T(1024)(128)(4,1)}), s8[2097152]{0:T(1024)(128)(4,1)S(1)}, s32[]{:S(2)}) async-start(s8[10485760]{0:T(1024)(128)(4,1)} %bitcast.401), calls=%async_computation.19 | async-start | bytes 4194304
  1515.0 98.7 %all-to-all-start.1 = ((bf16[1,4,512,2048]{3,2,0,1:T(8,128)(2,1)}), bf16[1,4,512,2048]{3,2,0,1:T(8,128)(2,1)}, u32[]{:S(2)}, u32[]{:S(2)}) async-start(bf16[1,4,512,2048]{3,2,0,1:T(8,128)(2,1)} %bitcast.389), calls=%async_computation.1 | async-start | bytes 16777216 | tf_op jit(solution)/shard_map/all_to_all | solution.py:45
  (16 other events, 161.9 us)
Sparse Core Ops, SparseCore 0:
  8.9 45.6 all-gather.26
  56.2 58.4 all-gather.22
  116.2 58.4 all-gather.18
  176.2 321.1 all-gather.28
  498.8 182.2 all-gather.30
  682.5 323.3 all-gather.34
  1007.5 59.6 all-gather.24
  1068.8 44.4 all-gather.32
  1114.8 180.9 all-gather.36
  1297.2 82.4 all-gather.20
where the time goes:
time: 1640 us; the launch traced here: 1630 us
  waiting for transfers between devices  912 us (56%)
  matrix products  454 us (28%)
  other arithmetic  160 us (10%)
  local copies, waits for them, and re-layouts  37.2 us (2%)
  blocking collectives  32 us (2%)
  starting transfers between devices  24.5 us (1%)
    all_gather x2, waiting for transfers between devices, local_fn(): w_in_loc = lax.all_gather(w_in_blk[layer_idx], 'data', axis=0, tiled=True)  363 us
    all_gather x4, waiting for transfers between devices, layer_block(): h_all = lax.all_gather(h_loc, 'model', axis=1, tiled=True)  203 us
    all_gather x2, waiting for transfers between devices, local_fn(): w_out_loc = lax.all_gather(w_out_blk[layer_idx], 'data', axis=1, tiled=True)  192 us
    dot_general x4, matrix products, layer_block(): jnp.einsum('btd,dhc->bthc', h_all, w_in3, preferred_element_type=jnp.floa...  187 us
    all_to_all x4, waiting for transfers between devices, layer_block(): lax.all_to_all(group_sum.reshape(n_seqs, n_model, t_loc, d_model), 'model...  152 us
    dot_general x4, matrix products, layer_block(): jnp.einsum('bthc,hcd->btd', joined, w_out3, preferred_element_type=jnp.fl...  105 us
    dot_general x4, matrix products, attention(): jnp.einsum('bhqk,bkc->bqhc', attn_probs, v_all, preferred_element_type=jn...  66 us
    reduce_sum x4, other arithmetic, attention(): attn_probs = jax.nn.softmax(scores, axis=-1).astype(jnp.bfloat16)  63.7 us
  transfers between devices with their start and end apart: 14, of which 10 were waited for; matrix products, arithmetic and copies ran while one was open for 38% of the time, Pallas kernels for 0%

commit v1 on v0

v1 whole, which is shorter than its diff:
```python
import functools
import math
import jax
import jax.numpy as jnp
from jax import lax
from jax.experimental import pallas as pl
from jax.experimental.pallas import tpu as pltpu
from jax.sharding import PartitionSpec as P

NORM_EPS = 1e-6
NEG_BIG = -1e30
BF16 = jnp.bfloat16
F32 = jnp.float32
VMEM_LIMIT = 67_000_000


def _params(n_axes):
    return pltpu.CompilerParams(dimension_semantics=("arbitrary",) * n_axes, vmem_limit_bytes=VMEM_LIMIT)


def _cost(flops, nbytes, trans=0):
    return pl.CostEstimate(flops=int(flops), bytes_accessed=int(nbytes), transcendentals=int(trans))


def _nbytes(*arrays):
    return sum(math.prod(a.shape) * a.dtype.itemsize for a in arrays)


def _norm_rows(x_f32, gain_row):
    centered = x_f32 - jnp.mean(x_f32, axis=-1, keepdims=True)
    variance = jnp.mean(centered * centered, axis=-1, keepdims=True)
    return (centered * lax.rsqrt(variance + NORM_EPS) * gain_row.astype(F32)).astype(BF16)


def _ln_kernel(x_ref, gain_ref, h_ref):
    h_ref[...] = _norm_rows(x_ref[...].astype(F32), gain_ref[...])


def layer_norm(x_blk, micro, gain):
    _, _, t_loc, d = x_blk.shape
    rows = min(128, t_loc)
    return pl.pallas_call(
        _ln_kernel,
        grid=(t_loc // rows,),
        in_specs=[
            pl.BlockSpec((None, None, rows, d), lambda r: (micro, 0, r, 0)),
            pl.BlockSpec((1, d), lambda r: (0, 0)),
        ],
        out_specs=pl.BlockSpec((rows, d), lambda r: (r, 0)),
        out_shape=jax.ShapeDtypeStruct((t_loc, d), BF16),
        compiler_params=_params(1),
        cost_estimate=_cost(t_loc * d * 8, t_loc * d * 4),
        name="ln",
    )(x_blk, gain)


def _sum_z(x, z_refs, z_dim):
    half = z_refs[0].shape[-1]
    n_half = half // z_dim
    parts = []
    for blk in range(n_half):
        for side in range(2):
            total = None
            for src in range(4):
                term = z_refs[2 * src + side][:, blk * z_dim:(blk + 1) * z_dim].astype(F32)
                total = term if total is None else total + term
            parts.append(total)
    return (x.astype(F32) + jnp.concatenate(parts, axis=-1)).astype(BF16)


def _combine_kernel(z_dim, x_ref, *refs):
    z_refs, gain_ref, y_ref, h_ref = refs[:8], refs[8], refs[9], refs[10]
    y = _sum_z(x_ref[...], z_refs, z_dim)
    y_ref[...] = y
    h_ref[...] = _norm_rows(y.astype(F32), gain_ref[...])


def combine(x_blk, micro, z_list, gain, z_dim):
    _, _, t_loc, d = x_blk.shape
    rows = min(128, t_loc)
    z_spec = pl.BlockSpec((rows, d // 2), lambda r: (r, 0))
    row_spec = pl.BlockSpec((rows, d), lambda r: (r, 0))
    return pl.pallas_call(
        functools.partial(_combine_kernel, z_dim),
        grid=(t_loc // rows,),
        in_specs=[pl.BlockSpec((None, None, rows, d), lambda r: (micro, 0, r, 0))] + [z_spec] * 8
        + [pl.BlockSpec((1, d), lambda r: (0, 0))],
        out_specs=[row_spec, row_spec],
        out_shape=[jax.ShapeDtypeStruct((t_loc, d), BF16)] * 2,
        compiler_params=_params(1),
        cost_estimate=_cost(t_loc * d * 16, t_loc * d * 14),
        name="combine",
    )(x_blk, *z_list, gain)


def _final_kernel(z_dim, x_ref, *refs):
    refs[-1][...] = _sum_z(x_ref[...], refs[:8], z_dim)


def final_combine(x, micro, n_micro, z_list, z_dim, prior):
    t_loc, d = x.shape
    rows = min(128, t_loc)
    z_spec = pl.BlockSpec((rows, d // 2), lambda r: (r, 0))
    extra = [] if prior is None else [prior]
    return pl.pallas_call(
        functools.partial(_final_kernel, z_dim),
        grid=(t_loc // rows,),
        in_specs=[pl.BlockSpec((rows, d), lambda r: (r, 0))] + [z_spec] * 8
        + [pl.BlockSpec(memory_space=pl.ANY)] * len(extra),
        out_specs=pl.BlockSpec((None, None, rows, d), lambda r: (micro, 0, r, 0)),
        out_shape=jax.ShapeDtypeStruct((n_micro, 1, t_loc, d), BF16),
        input_output_aliases={} if prior is None else {9: 0},
        compiler_params=_params(1),
        cost_estimate=_cost(t_loc * d * 8, t_loc * d * 12),
        name="final",
    )(x, *z_list, *extra)


def _pick_kernel(idx_ref, src_ref, dst_ref):
    dst_ref[...] = src_ref[...]


def pick_blocks(idx, gathered):
    n_z, rows, cols = gathered.shape
    return pl.pallas_call(
        _pick_kernel,
        grid_spec=pltpu.PrefetchScalarGridSpec(
            num_scalar_prefetch=1,
            grid=(n_z - 1,),
            in_specs=[pl.BlockSpec((1, rows, cols), lambda j, s: (lax.rem(s[0] + 1 + j, n_z), 0, 0))],
            out_specs=pl.BlockSpec((1, rows, cols), lambda j, s: (j, 0, 0)),
        ),
        out_shape=jax.ShapeDtypeStruct((n_z - 1, rows, cols), BF16),
        compiler_params=_params(1),
        cost_estimate=_cost(rows * cols, 4 * (n_z - 1) * rows * cols),
        name="pick",
    )(idx, gathered)


def _take_kernel(idx_ref, *refs):
    out_ref = refs[-1]
    if len(refs) == 2:
        out_ref[...] = refs[0][0]
    else:
        at = 0
        for src in refs[:-1]:
            out_ref[:, at:at + src.shape[2]] = src[0]
            at += src.shape[2]


def take_blocks(idx, sources, steps):
    rows = sources[0][1][1]
    cols = sum(src[1][2] for src in sources)
    return pl.pallas_call(
        _take_kernel,
        grid_spec=pltpu.PrefetchScalarGridSpec(
            num_scalar_prefetch=1,
            grid=(steps,),
            in_specs=[pl.BlockSpec(shape, index) for _, shape, index in sources],
            out_specs=pl.BlockSpec((rows, cols), lambda t, s: (0, t)),
        ),
        out_shape=jax.ShapeDtypeStruct((rows, cols * steps), BF16),
        compiler_params=_params(1),
        cost_estimate=_cost(rows * cols * steps, 4 * rows * cols * steps),
        name="take",
    )(idx, *[src[0] for src in sources])


def _proj_kernel(gated, tile, kinds, n_h, *refs):
    h_refs = refs[:n_h]
    at = n_h
    w_refs = []
    for kind in kinds:
        width = 3 if kind[1] else 1
        w_refs.append(refs[at:at + width])
        at += width
    n_out = 1 if gated else 2
    outs = refs[at:at + n_out]
    h_scr, w_scr, o_scr, h_sems, w_sems, o_sems = refs[at + n_out:]
    step, last = pl.program_id(0), pl.num_programs(0) - 1
    n_pair, t_loc = n_h // 2, h_scr.shape[1] // 2
    part, z_idx = lax.axis_index("part"), lax.axis_index("data")
    h_copies = [pltpu.make_async_copy(src, h_scr.at[i // 2, pl.ds((i % 2) * t_loc, t_loc)], h_sems.at[i]) for i, src in enumerate(h_refs)]

    def load(at_step):
        slot = lax.rem(at_step, 2)
        start = 0
        for (steps, place), refs_c in zip(kinds, w_refs):
            begin = start

            @pl.when((at_step >= begin) & (at_step < begin + steps))
            def _():
                n = at_step - begin
                cols = pl.ds(pl.multiple_of(n * 2 * tile, 2 * tile), 2 * tile)
                src = refs_c[0]
                n_blk, z_dim, _ = src.shape
                for j in range(n_blk):
                    blk = lax.rem(z_idx + 1 + j, n_blk + 1) if place else j
                    rows = pl.ds(pl.multiple_of(blk * z_dim, z_dim), z_dim)
                    pltpu.make_async_copy(src.at[j, :, cols], w_scr.at[slot, rows], w_sems.at[slot]).start()
                if place:
                    layer, sides = place
                    rows = pl.ds(pl.multiple_of(z_idx * z_dim, z_dim), z_dim)
                    for side in range(2):
                        first = jnp.where(part == 0, sides[side][0], sides[side][1]) + n * tile
                        own = refs_c[1 + side].at[layer, :, pl.ds(pl.multiple_of(first, tile), tile)]
                        pltpu.make_async_copy(own, w_scr.at[slot, rows, pl.ds(side * tile, tile)], w_sems.at[slot]).start()

            start += steps

    def out_copies(at_step, pair):
        slot = lax.rem(at_step, 2)
        cols = pl.ds(pl.multiple_of(at_step * tile, tile), tile)
        return [pltpu.make_async_copy(o_scr.at[slot, k, pl.ds(2 * pair, 2)], out.at[pl.ds(2 * pair, 2), :, cols], o_sems.at[slot, pair]) for k, out in enumerate(outs)]

    @pl.when(step == 0)
    def _():
        load(step)
        for copy in h_copies:
            copy.start()

    @pl.when(step < last)
    def _():
        load(step + 1)

    slot = lax.rem(step, 2)
    pltpu.make_async_copy(w_scr.at[slot], w_scr.at[slot], w_sems.at[slot]).wait()
    for pair in range(n_pair):
        @pl.when(step == 0)
        def _():
            h_copies[2 * pair].wait()
            h_copies[2 * pair + 1].wait()

        @pl.when(step >= 2)
        def _():
            for copy in out_copies(step - 2, pair):
                copy.wait()

        acc = jnp.dot(h_scr[pair], w_scr[slot], preferred_element_type=F32)
        left, right = acc[:, :tile].astype(BF16), acc[:, tile:].astype(BF16)
        shape = (2, t_loc, tile)
        if gated:
            o_scr[slot, 0, pl.ds(2 * pair, 2)] = (jax.nn.silu(left.astype(F32)) * right.astype(F32)).astype(BF16).reshape(shape)
        else:
            o_scr[slot, 0, pl.ds(2 * pair, 2)] = left.reshape(shape)
            o_scr[slot, 1, pl.ds(2 * pair, 2)] = right.reshape(shape)
        for copy in out_copies(step, pair):
            copy.start()

    @pl.when(step == last)
    def _():
        for pair in range(n_pair):
            @pl.when(step >= 1)
            def _():
                for copy in out_copies(step - 1, pair):
                    copy.wait()

            for copy in out_copies(step, pair):
                copy.wait()


def project(pieces, chunks, gated, tile):
    t_loc, d = pieces[0].shape
    n_piece = len(pieces)
    args, kinds, steps = [], [], 0
    for array, *own in chunks:
        n = array.shape[2] // (2 * tile)
        kinds.append((n, own[2] if own else None))
        args += [array] + own[:2]
        steps += n
    n_out = 1 if gated else 2
    out = pl.pallas_call(
        functools.partial(_proj_kernel, gated, tile, tuple(kinds), n_piece),
        grid=(steps,),
        in_specs=[pl.BlockSpec(memory_space=pl.ANY)] * (n_piece + len(args)),
        out_specs=[pl.BlockSpec(memory_space=pl.ANY)] * n_out,
        scratch_shapes=[
            pltpu.VMEM((n_piece // 2, 2 * t_loc, d), BF16),
            pltpu.VMEM((2, d, 2 * tile), BF16),
            pltpu.VMEM((2, n_out, n_piece, t_loc, tile), BF16),
            pltpu.SemaphoreType.DMA((n_piece,)),
            pltpu.SemaphoreType.DMA((2,)),
            pltpu.SemaphoreType.DMA((2, n_piece // 2)),
        ],
        out_shape=[jax.ShapeDtypeStruct((n_piece, t_loc, steps * tile), BF16)] * n_out,
        compiler_params=_params(1),
        cost_estimate=_cost(4 * n_piece * t_loc * d * steps * tile, _nbytes(*pieces) + 4 * d * steps * tile + 2 * n_out * n_piece * t_loc * steps * tile),
        name="proj_gated" if gated else "proj_qkv",
    )(*pieces, *args)
    return out[0] if gated else out


def _attn_kernel(idx_ref, len_ref, *refs):
    q_a, q_b, kv_a, kv_b, o_ref, k_scr, v_scr, s_scr, p_scr = refs
    head, slot, row = pl.program_id(0), pl.program_id(1), pl.program_id(2)
    part, me = idx_ref[1], idx_ref[2]
    n_blk, blk, head_dim = kv_a.shape
    bq = q_a.shape[1]

    @pl.when((head == 0) & (slot == 0) & (row == 0))
    def _():
        for k in range(n_blk):
            rows = pl.ds(pl.multiple_of((me ^ k) * blk, blk), blk)
            first, second = kv_a[k], kv_b[k]
            k_scr[rows, :] = jnp.where(part == 0, first, second)
            v_scr[rows, :] = jnp.where(part == 0, second, first)

    q = jnp.where(head == 0, q_a[0], q_b[0])
    q_blk = me ^ slot
    seq_len = len_ref[0]
    n_keys = jnp.minimum(q_blk + 1, (seq_len + blk - 1) // blk)
    rate = math.log2(math.e) / math.sqrt(head_dim)
    lane = min(128, blk)

    def fold(x, op):
        total = x[:, :lane]
        for i in range(1, x.shape[1] // lane):
            total = op(total, x[:, i * lane:(i + 1) * lane])
        return total

    for n in range(1, n_blk + 1):
        @pl.when(n_keys == n)
        def _():
            top = None
            for j in range(n):
                s = lax.dot_general(q, k_scr[j * blk:(j + 1) * blk, :], (((1,), (1,)), ((), ())), preferred_element_type=F32)
                if j == n - 1:
                    q_pos = q_blk * blk + row * bq + lax.broadcasted_iota(jnp.int32, (bq, blk), 0)
                    k_pos = j * blk + lax.broadcasted_iota(jnp.int32, (bq, blk), 1)
                    s = jnp.where(k_pos <= jnp.minimum(q_pos, seq_len - 1), s, NEG_BIG)
                s_scr[:, j * blk:(j + 1) * blk] = s
                part_top = fold(s, jnp.maximum)
                top = part_top if top is None else jnp.maximum(top, part_top)
            top = jnp.max(top, axis=-1, keepdims=True)
            total = None
            for j in range(n):
                e = jnp.exp2((s_scr[:, j * blk:(j + 1) * blk] - top) * rate)
                s_scr[:, j * blk:(j + 1) * blk] = e
                part_sum = fold(e, jnp.add)
                total = part_sum if total is None else total + part_sum
            inv = 1.0 / jnp.sum(total, axis=-1, keepdims=True)
            for j in range(n):
                p_scr[:, j * blk:(j + 1) * blk] = (s_scr[:, j * blk:(j + 1) * blk] * inv).astype(BF16)
            o_ref[0] = jnp.dot(p_scr[:, :n * blk], v_scr[:n * blk, :], preferred_element_type=F32).astype(BF16)


def attention(idx, seq_len, q_a, q_b, kv_a, kv_b):
    head_dim = q_a[3]
    _, blk, _ = q_a[0].shape
    n_blk = 4
    bq = min(256, blk)
    n_row = blk // bq

    def q_spec(item, which):
        _, col, first, _ = item
        hold = 0 if which else n_blk - 1, 0 if which else n_row - 1
        return pl.BlockSpec((1, bq, head_dim), lambda a, k, r, s, t: (first + jnp.where(a == which, k, hold[0]), jnp.where(a == which, r, hold[1]), col))

    def kv_spec(item):
        _, col, first, _ = item
        return pl.BlockSpec((n_blk, blk, head_dim), lambda a, k, r, s, t: (first // n_blk, 0, col))

    return pl.pallas_call(
        _attn_kernel,
        grid_spec=pltpu.PrefetchScalarGridSpec(
            num_scalar_prefetch=2,
            grid=(2, n_blk, n_row),
            in_specs=[q_spec(q_a, 0), q_spec(q_b, 1), kv_spec(kv_a), kv_spec(kv_b)],
            out_specs=pl.BlockSpec((1, bq, head_dim), lambda a, k, r, s, t: (n_blk * a + k, r, 0)),
            scratch_shapes=[
                pltpu.VMEM((n_blk * blk, head_dim), BF16),
                pltpu.VMEM((n_blk * blk, head_dim), BF16),
                pltpu.VMEM((bq, n_blk * blk), F32),
                pltpu.VMEM((bq, n_blk * blk), BF16),
            ],
        ),
        out_shape=jax.ShapeDtypeStruct((2 * n_blk, blk, head_dim), BF16),
        compiler_params=_params(3),
        cost_estimate=_cost(8 * (n_blk * blk) ** 2 * head_dim * 0.8, 12 * n_blk * blk * head_dim, (n_blk * blk) ** 2),
        name="attn",
    )(idx, seq_len, q_a[0], q_b[0], kv_a[0], kv_b[0])


def _out_kernel(layer, side, items, n_in, *refs):
    srcs = refs[:n_in]
    wa_ref, own_ref, rel_ref = refs[n_in:n_in + 3]
    z_refs = refs[n_in + 3:n_in + 7]
    j_scr, w_scr, z_scr, j_sems, w_sems, z_sems = refs[n_in + 7:]
    step, last = pl.program_id(0), pl.num_programs(0) - 1
    t_loc = j_scr.shape[1] // 2
    n_z, rows, width = wa_ref.shape
    part, z_idx = lax.axis_index("part"), lax.axis_index("data")
    order = (2, 3, 0, 1)
    copies = []
    for i, slot in enumerate(order):
        at, mine = 0, []
        for head in range(2):
            for low, high, first_low, first_high, col, size in items[head]:
                ref, first = (srcs[low], first_low) if slot < 2 else (srcs[high], first_high)
                src = ref.at[first + slot, :, pl.ds(col, size)]
                mine.append(pltpu.make_async_copy(src, j_scr.at[i // 2, pl.ds((i % 2) * t_loc, t_loc), pl.ds(at, size)], j_sems.at[i // 2]))
                at += size
        copies.append(mine)

    def load(at_step):
        for i in range(2):
            blk = 2 * at_step + i
            cols = pl.ds(i * width, width)
            pltpu.make_async_copy(wa_ref.at[blk], w_scr.at[at_step, pl.ds(0, rows), cols], w_sems.at[at_step]).start()
            below = w_scr.at[at_step, pl.ds(rows, rows), cols]

            @pl.when(blk == z_idx)
            def _():
                first = pl.multiple_of((1 - part) * rows, rows)
                pltpu.make_async_copy(own_ref.at[layer, pl.ds(first, rows), pl.ds(side * width, width)], below, w_sems.at[at_step]).start()

            @pl.when(blk != z_idx)
            def _():
                pltpu.make_async_copy(rel_ref.at[lax.rem(blk - z_idx - 1 + n_z, n_z)], below, w_sems.at[at_step]).start()

    def z_copies(at_step, pair):
        cols = pl.ds(pl.multiple_of(at_step * 2 * width, 2 * width), 2 * width)
        return [pltpu.make_async_copy(z_scr.at[at_step, pair, pl.ds(k * t_loc, t_loc)], z_refs[order[2 * pair + k]].at[:, cols], z_sems.at[at_step, pair]) for k in range(2)]

    @pl.when(step == 0)
    def _():
        load(0)
        for mine in copies[:2]:
            for copy in mine:
                copy.start()
        load(1)
        for mine in copies[2:]:
            for copy in mine:
                copy.start()

    pltpu.make_async_copy(w_scr.at[step], w_scr.at[step], w_sems.at[step]).wait()
    for pair in range(2):
        @pl.when(step == 0)
        def _():
            for mine in copies[2 * pair:2 * pair + 2]:
                for copy in mine:
                    copy.wait()

        z_scr[step, pair] = jnp.dot(j_scr[pair], w_scr[step], preferred_element_type=F32).astype(BF16)
        for copy in z_copies(step, pair):
            copy.start()

    @pl.when(step == last)
    def _():
        for at_step in range(2):
            for pair in range(2):
                for copy in z_copies(at_step, pair):
                    copy.wait()


def out_project(layer, side, items, srcs, w_a, w_own, w_rel):
    n_z, rows, z_dim = w_a.shape
    n_slot, t_loc = 4, srcs[0].shape[1]
    steps = n_z // 2
    return pl.pallas_call(
        functools.partial(_out_kernel, layer, side, items, len(srcs)),
        grid=(steps,),
        in_specs=[pl.BlockSpec(memory_space=pl.ANY)] * (len(srcs) + 3),
        out_specs=[pl.BlockSpec(memory_space=pl.ANY)] * n_slot,
        scratch_shapes=[
            pltpu.VMEM((n_slot // 2, 2 * t_loc, 2 * rows), BF16),
            pltpu.VMEM((steps, 2 * rows, 2 * z_dim), BF16),
            pltpu.VMEM((steps, n_slot // 2, 2 * t_loc, 2 * z_dim), BF16),
            pltpu.SemaphoreType.DMA((2,)),
            pltpu.SemaphoreType.DMA((steps,)),
            pltpu.SemaphoreType.DMA((steps, 2)),
        ],
        out_shape=[jax.ShapeDtypeStruct((t_loc, n_z * z_dim), BF16)] * n_slot,
        compiler_params=_params(1),
        cost_estimate=_cost(4 * n_slot * t_loc * rows * n_z * z_dim, 4 * n_slot * t_loc * rows + 4 * rows * n_z * z_dim + 2 * n_slot * t_loc * n_z * z_dim),
        name="out_proj",
    )(*srcs, w_a, w_own, w_rel)


def _swap(value, axis, size, k):
    return lax.ppermute(value, axis, [(i, i ^ k) for i in range(size)])


TAKE, PICK, GAIN, NORM, FORWARD, QKV, ATTEND, GATE, OUT, JOIN, FINAL = (
    "take", "pick", "gain", "norm", "forward", "qkv", "attend", "gate", "out", "join", "final")

ORDER = [
    (TAKE, "00"), (GAIN, ""), (NORM, "0"), (NORM, "1"), *[(TAKE, f"0{c}") for c in "1234"], *[(TAKE, f"1{c}") for c in "01234"],
    (FORWARD, "00"), (PICK, "00"), (QKV, "0", "0", "a"), (FORWARD, "01"), (QKV, "0", "0", "b"), (QKV, "0", "1", "a"), (PICK, "01"),
    (QKV, "0", "1", "b"), (ATTEND, "00"), (ATTEND, "01"), (GATE, "0", "01", "a0"), (PICK, "02"), (GATE, "0", "01", "b0"),
    (GATE, "0", "01", "a1"), (PICK, "03"), (GATE, "0", "01", "b1"), (PICK, "04"),
    (OUT, "000"), (PICK, "10"), (OUT, "001"), (OUT, "010"), (JOIN, "00"), (PICK, "11"), (OUT, "011"), (FORWARD, "10"),
    (QKV, "1", "0", "ab"), (ATTEND, "10"), (PICK, "12"), (GATE, "1", "0", "a0b0a1"), (JOIN, "01"), (PICK, "13"), (GATE, "1", "0", "b1"),
    (GATE, "1", "1", "a0b0a1b1", "lo"), (PICK, "14"), (OUT, "100"), (FORWARD, "11"), (QKV, "1", "1", "ab"), (ATTEND, "11"), (OUT, "101"),
    (GATE, "1", "1", "a0b0a1b1", "hi"), (OUT, "110"), (OUT, "111"), (FINAL, "0"), (FINAL, "1"),
]


def build(mesh):
    n_part, n_data, n_model = mesh.shape["part"], mesh.shape["data"], mesh.shape["model"]
    act_spec = P(None, ("part", "data"), "model", None)

    def local_fn(x_blk, len_blk, gain_blk, w_in_blk, w_kv_blk, w_out_blk):
        n_micro, _, t_loc, d = x_blk.shape
        n_layers, z_dim, in_loc = w_in_blk.shape
        head_dim = w_kv_blk.shape[2] // 2
        unit_out = w_out_blk.shape[1] // 2
        ff = unit_out - head_dim
        unit_in = in_loc // 2
        n_chunk = 2
        ff_c = ff // n_chunk
        tile = min(256, ff_c)
        per_chunk = ff_c // tile
        z_half = z_dim // 2
        z_idx = lax.axis_index("data")
        idx = jnp.stack([z_idx, lax.axis_index("part"), lax.axis_index("model")]).astype(jnp.int32)

        now = [idx]

        def seq(value):
            now[0], value = lax.optimization_barrier((now[0], value))
            return value

        def tied(value):
            return lax.optimization_barrier((value, now[0]))[0]

        def q_map(layer):
            return lambda n, s: (layer, 0, s[1] * (unit_in // head_dim))

        def kv_map(layer):
            return lambda n, s: (layer, 0, s[1])

        def gate_map(layer, c, up):
            return lambda n, s: (layer, 0, (s[1] * unit_in + head_dim + (ff if up else 0) + c * ff_c) // tile + n)

        def out_map(layer, side):
            return lambda n, s: (layer, s[1], side)

        gathered, rel = {}, {}

        def take(at):
            layer, c = map(int, at)
            if c == 0:
                sources = [(w_in_blk, (1, z_dim, head_dim), q_map(layer)), (w_kv_blk, (1, z_dim, head_dim), kv_map(layer))]
                steps = 1
            elif c <= n_chunk:
                sources = [(w_in_blk, (1, z_dim, tile), gate_map(layer, c - 1, up)) for up in (False, True)]
                steps = per_chunk
            else:
                sources = [(w_out_blk, (1, unit_out, z_half), out_map(layer, c - 1 - n_chunk))]
                steps = 1
            mine = seq(take_blocks(now[0], sources, steps))
            gathered[layer, c] = lax.all_gather(mine, "data", axis=0)

        def pick(at):
            layer, c = map(int, at)
            send = seq(pick_blocks(now[0], gathered[layer, c]))
            rel[layer, c] = _swap(send, "part", n_part, 1)

        hs, near, far, both = {}, {}, {}, {}

        def spread(layer, m, h):
            hs[layer, m] = h
            far[layer, m] = _swap(h, "model", n_model, 2)
            near[layer, m] = _swap(h, "model", n_model, 1)

        def forward(at):
            layer, m = map(int, at)
            far[layer, m] = seq(far[layer, m])
            both[layer, m] = _swap(far[layer, m], "model", n_model, 1)

        q, kv, attn, mid, zs = {}, {}, {}, {}, {}

        def pieces(layer, micros, slots="lohi"):
            found = []
            for m in map(int, micros):
                found += [hs[layer, m], near[layer, m]] if "lo" in slots else []
                found += [far[layer, m], both[layer, m]] if "hi" in slots else []
            return [tied(found[0])] + found[1:]

        def qkv(layer, micros, names):
            layer = int(layer)
            chunks = []
            for name in names:
                if name == "a":
                    chunks.append((gathered[layer, 0],))
                else:
                    chunks.append((rel[layer, 0], w_in_blk, w_kv_blk, (layer, ((unit_in, 0), (head_dim, 0)))))
            q_out, kv_out = seq(project(pieces(layer, micros), chunks, False, head_dim))
            for i, m in enumerate(map(int, micros)):
                for col, name in enumerate(names):
                    q[layer, m, name] = (q_out, col, n_model * i, head_dim)
                    kv[layer, m, name] = (kv_out, col, n_model * i, head_dim)

        def attend(at):
            layer, m = map(int, at)
            attn[layer, m] = seq(attention(now[0], len_blk[m], q[layer, m, "a"], q[layer, m, "b"], kv[layer, m, "a"], kv[layer, m, "b"]))

        def gate(layer, micros, names, slots="lohi"):
            layer = int(layer)
            chunks = []
            names = [names[i:i + 2] for i in range(0, len(names), 2)]
            for head, c in names:
                c = int(c)
                if head == "a":
                    chunks.append((gathered[layer, 1 + c],))
                else:
                    gate_at = head_dim + c * ff_c
                    up_at = gate_at + ff
                    chunks.append((rel[layer, 1 + c], w_in_blk, w_in_blk, (layer, ((unit_in + gate_at, gate_at), (unit_in + up_at, up_at)))))
            got = seq(project(pieces(layer, micros, slots), chunks, True, tile))
            for i, m in enumerate(map(int, micros)):
                for col, name in enumerate(names):
                    for part_of in ("lo", "hi"):
                        if part_of in slots:
                            first = n_model * i if slots == "lohi" else (0 if slots == "lo" else -2)
                            mid[layer, m, name, part_of] = (got, first, col * ff_c)

        def out(at):
            layer, m, side = map(int, at)
            c = 1 + n_chunk + side
            srcs = [tied(attn[layer, m])]

            def operand(array):
                for i, known in enumerate(srcs):
                    if known is array:
                        return i
                srcs.append(array)
                return len(srcs) - 1

            items = []
            for number, head in enumerate("ab"):
                row = [(0, 0, n_model * number, n_model * number, 0, head_dim)]
                for i in range(n_chunk):
                    low, high = mid[layer, m, f"{head}{i}", "lo"], mid[layer, m, f"{head}{i}", "hi"]
                    row.append((operand(low[0]), operand(high[0]), low[1], high[1], low[2], ff_c))
                items.append(tuple(row))
            values = seq(out_project(layer, side, tuple(items), srcs, gathered[layer, c], w_out_blk, rel[layer, c]))
            for k in (0, 2, 3, 1):
                zs[layer, m, k, side] = values[k] if k == 0 else _swap(values[k], "model", n_model, k)

        ys = {}

        def z_list(layer, m):
            return [zs[layer, m, k, side] for k in range(n_model) for side in range(2)]

        gain_full = [None]

        def gain(_):
            blk = tied(gain_blk)
            got = [blk] + [_swap(blk, "data", n_data, k) for k in range(1, n_data)]
            blocks = []
            for b in range(n_data):
                choice = got[n_data - 1]
                for k in range(n_data - 1):
                    choice = jnp.where((z_idx ^ k) == b, got[k], choice)
                blocks.append(choice)
            gain_full[0] = jnp.concatenate(blocks, axis=1)

        def join(at):
            layer, m = map(int, at)
            src, place = (x_blk, m) if layer == 0 else (ys[layer - 1, m].reshape(1, 1, t_loc, d), 0)
            row = tied(gain_full[0][layer + 1:layer + 2])
            ys[layer, m], h = seq(combine(src, place, z_list(layer, m), row, z_half))
            spread(layer + 1, m, h)

        def norm(at):
            m = int(at)
            spread(0, m, seq(layer_norm(x_blk, m, tied(gain_full[0][0:1]))))

        result = [None]

        def final(at):
            m = int(at)
            result[0] = seq(final_combine(ys[n_layers - 2, m], m, n_micro, z_list(n_layers - 1, m), z_half, result[0]))

        steps = {TAKE: take, PICK: pick, GAIN: gain, NORM: norm, FORWARD: forward, QKV: qkv, ATTEND: attend, GATE: gate, OUT: out, JOIN: join, FINAL: final}
        for step in ORDER:
            steps[step[0]](*step[1:])
        return result[0]

    return jax.shard_map(
        local_fn,
        mesh=mesh,
        in_specs=(act_spec, P(None, ("part", "data")), P(None, "data"), P(None, "data", "model"), P(None, "data", None), P(None, "model", "data")),
        out_specs=act_spec,
        check_vma=False,
    )


def solution(mesh):
    return build(mesh)
```

time: 1640 us -> 1150 us (0.70)
  Pallas kernels: 0 us -> 581 us
  matrix products: 454 us -> 0 us
  waiting for transfers between devices: 912 us -> 502 us
  other arithmetic: 160 us -> 0.64 us
  local copies, waits for them, and re-layouts: 37.2 us -> 1.17 us
  blocking collectives: 32 us -> 0 us
    all_gather x10, waiting for transfers between devices: 758 us -> 0.13 us  [take(): gathered[layer, c] = lax.all_gather(mine, 'data', axis=0)]
    pallas_call x0 -> x52, Pallas kernels: none -> 581 us  [the longest x14 247 us: project(): pl.pallas_call(functools.partial(_proj_kernel, gated, tile, tuple(kinds),...]
    ppermute x0 -> x49, waiting for transfers between devices: none -> 502 us  [_swap(): return lax.ppermute(value, axis, [(i, i ^ k) for i in range(size)])]
    dot_general x20 -> x0, matrix products: 454 us -> none  [the longest x4 187 us: layer_block(): jnp.einsum('btd,dhc->bthc', h_all, w_in3, preferred_element_type=jnp.floa...]
    all_to_all x4 -> x0, waiting for transfers between devices: 152 us -> none  [layer_block(): lax.all_to_all(group_sum.reshape(n_seqs, n_model, t_loc, d_model), 'model...]
    reduce_sum x12 -> x0, other arithmetic: 101 us -> none  [the longest x4 63.7 us: attention(): attn_probs = jax.nn.softmax(scores, axis=-1).astype(jnp.bfloat16)]
    convert_element_type x10 -> x0, other arithmetic: 47.2 us -> none  [the longest x4 35.3 us: layer_block(): (jax.nn.silu(gate_act.astype(jnp.float32)) * up_act.astype(jnp.float32))....]
    ppermute x0 -> x49, starting transfers between devices: none -> 34.8 us  [_swap(): return lax.ppermute(value, axis, [(i, i ^ k) for i in range(size)])]
  transfers between devices with their start and end apart: 14 -> 59, of which waited for: 10 -> 26; matrix products, arithmetic and copies ran while one was open for 38% -> 0% of each run, Pallas kernels for 0% -> 50%
where the time goes in v1:
time: 1150 us; the launch traced here: 1130 us
  Pallas kernels  581 us (51%)
  waiting for transfers between devices  502 us (44%)
  starting transfers between devices  35.2 us (3%)
  between operations  14.4 us (1%)
    ppermute x49, waiting for transfers between devices, _swap(): return lax.ppermute(value, axis, [(i, i ^ k) for i in range(size)])  502 us
    pallas_call x14, Pallas kernels, project(): pl.pallas_call(functools.partial(_proj_kernel, gated, tile, tuple(kinds),...  247 us
    pallas_call x8, Pallas kernels, out_project(): pl.pallas_call(functools.partial(_out_kernel, layer, side, items, len(src...  131 us
    pallas_call x4, Pallas kernels, attention(): pl.pallas_call(_attn_kernel, grid_spec=pltpu.PrefetchScalarGridSpec(num_s...  93.1 us
    pallas_call x10, Pallas kernels, pick_blocks(): pl.pallas_call(_pick_kernel, grid_spec=pltpu.PrefetchScalarGridSpec(num_s...  46.4 us
    ppermute x49, starting transfers between devices, _swap(): return lax.ppermute(value, axis, [(i, i ^ k) for i in range(size)])  34.8 us
    pallas_call x10, Pallas kernels, take_blocks(): pl.pallas_call(_take_kernel, grid_spec=pltpu.PrefetchScalarGridSpec(num_s...  26.9 us
  transfers between devices with their start and end apart: 59, of which 26 were waited for; matrix products, arithmetic and copies ran while one was open for 0% of the time, Pallas kernels for 50%

profile of v1, /device:TPU:8, one launch (start us, length us, event | category | flops | bytes accessed | tf_op | source)
XLA Modules:
  0.0 1134.7 jit_solution(7882338327160379257)
XLA Ops:
  52.5 36.2 %collective-permute-done.3.refs_2_ = bf16[512,2048]{1,0:T(8,128)(2,1)} collective-permute-done((bf16[512,2048]{1,0:T(8,128)(2,1)}, bf16[512,2048]{1,0:T(8,128)(2,1)}, u32[]{:S(2)}, u32[]{:S(2)}) %collective-permute-start.3) | collective-permute-done | bytes 2097184 | tf_op jit(solution)/shard_map/ppermute | solution.py:481
  103.7 33.3 %collective-permute-done.6.refs_2_.refs_6_ = bf16[512,2048]{1,0:T(8,128)(2,1)} collective-permute-done((bf16[512,2048]{1,0:T(8,128)(2,1)}, bf16[512,2048]{1,0:T(8,128)(2,1)}, u32[]{:S(2)}, u32[]{:S(2)}) %collective-permute-start.6) | collective-permute-done | bytes 2097184 | tf_op jit(solution)/shard_map/ppermute | solution.py:481
  139.2 35.0 %collective-permute-done.7.refs_4_ = bf16[3,512,512]{2,1,0:T(8,128)(2,1)} collective-permute-done((bf16[3,512,512]{2,1,0:T(8,128)(2,1)}, bf16[3,512,512]{2,1,0:T(8,128)(2,1)}, u32[]{:S(2)}, u32[]{:S(2)}) %collective-permute-start.7) | collective-permute-done | bytes 1572896 | tf_op jit(solution)/shard_map/ppermute | solution.py:481
  209.7 23.3 %attn.4.refs_0_ = bf16[8,512,256]{2,1,0:T(8,128)(2,1)} custom-call(s32[3]{0:T(128)} %pad_add_fusion.idx_ref, s32[1]{0:T(128)} %bitcast.5.len_ref, bf16[4,512,256]{2,1,0:T(8,128)(2,1)} %get-tuple-element.261.refs_0_, bf16[4,512,256]{2,1,0:T(8,128)(2,1)} %get-tuple-element.262.refs_1_, bf16[4,512,256]{2,1,0:T(8,128)(2,1)} %get-tuple-element.263.refs_2_, ...), custom_call_target="tpu_custom_call" | custom-call | flops 6871947776 | bytes 6291456 | tf_op jit(solution)/shard_map/attn/pallas_call | solution.py:363
  232.9 23.2 %attn.5.refs_0_ = bf16[8,512,256]{2,1,0:T(8,128)(2,1)} custom-call(s32[3]{0:T(128)} %pad_add_fusion.idx_ref, s32[1]{0:T(128)} %bitcast.6.len_ref, bf16[4,512,256]{2,1,0:T(8,128)(2,1)} %get-tuple-element.266.refs_0_, bf16[4,512,256]{2,1,0:T(8,128)(2,1)} %get-tuple-element.267.refs_1_, bf16[4,512,256]{2,1,0:T(8,128)(2,1)} %get-tuple-element.268.refs_2_, ...), custom_call_target="tpu_custom_call" | custom-call | flops 6871947776 | bytes 6291456 | tf_op jit(solution)/shard_map/attn/pallas_call | solution.py:363
  256.2 22.9 %proj_gated.8.refs_1_ = bf16[8,512,512]{2,1,0:T(8,128)(2,1)} custom-call(bf16[512,2048]{1,0:T(8,128)(2,1)} %ln.2.refs_0_, bf16[512,2048]{1,0:T(8,128)(2,1)} %collective-permute-done.4.refs_1_, bf16[512,2048]{1,0:T(8,128)(2,1)} %collective-permute-done.3.refs_2_, bf16[512,2048]{1,0:T(8,128)(2,1)} %collective-permute-done.5.refs_3_, ...), custom_call_target="tpu_custom_call" | custom-call | flops 17179869184 | bytes 25165824 | tf_op jit(solution)/shard_map/proj_gated/pallas_call | solution.py:272
  284.4 22.5 %proj_gated.9.refs_3_ = bf16[8,512,512]{2,1,0:T(8,128)(2,1)} custom-call(bf16[512,2048]{1,0:T(8,128)(2,1)} %ln.2.refs_0_, bf16[512,2048]{1,0:T(8,128)(2,1)} %collective-permute-done.4.refs_1_, bf16[512,2048]{1,0:T(8,128)(2,1)} %collective-permute-done.3.refs_2_, bf16[512,2048]{1,0:T(8,128)(2,1)} %collective-permute-done.5.refs_3_, ...), custom_call_target="tpu_custom_call" | custom-call | flops 17179869184 | bytes 25165824 | tf_op jit(solution)/shard_map/proj_gated/pallas_call | solution.py:272
  306.9 22.7 %proj_gated.10.refs_2_ = bf16[8,512,512]{2,1,0:T(8,128)(2,1)} custom-call(bf16[512,2048]{1,0:T(8,128)(2,1)} %ln.2.refs_0_, bf16[512,2048]{1,0:T(8,128)(2,1)} %collective-permute-done.4.refs_1_, bf16[512,2048]{1,0:T(8,128)(2,1)} %collective-permute-done.3.refs_2_, bf16[512,2048]{1,0:T(8,128)(2,1)} %collective-permute-done.5.refs_3_, ...), custom_call_target="tpu_custom_call" | custom-call | flops 17179869184 | bytes 25165824 | tf_op jit(solution)/shard_map/proj_gated/pallas_call | solution.py:272
  355.6 22.6 %proj_gated.11.refs_4_ = bf16[8,512,512]{2,1,0:T(8,128)(2,1)} custom-call(bf16[512,2048]{1,0:T(8,128)(2,1)} %ln.2.refs_0_, bf16[512,2048]{1,0:T(8,128)(2,1)} %collective-permute-done.4.refs_1_, bf16[512,2048]{1,0:T(8,128)(2,1)} %collective-permute-done.3.refs_2_, bf16[512,2048]{1,0:T(8,128)(2,1)} %collective-permute-done.5.refs_3_, ...), custom_call_target="tpu_custom_call" | custom-call | flops 17179869184 | bytes 25165824 | tf_op jit(solution)/shard_map/proj_gated/pallas_call | solution.py:272
  418.4 19.9 %collective-permute-done.13.refs_7_ = bf16[3,1280,256]{2,1,0:T(8,128)(2,1)} collective-permute-done((bf16[3,1280,256]{2,1,0:T(8,128)(2,1)}, bf16[3,1280,256]{2,1,0:T(8,128)(2,1)}, u32[]{:S(2)}, u32[]{:S(2)}) %collective-permute-start.13) | collective-permute-done | bytes 1966112 | tf_op jit(solution)/shard_map/ppermute | solution.py:481
  481.1 22.5 %collective-permute-done.17.refs_5_ = bf16[512,1024]{1,0:T(8,128)(2,1)} collective-permute-done((bf16[512,1024]{1,0:T(8,128)(2,1)}, bf16[512,1024]{1,0:T(8,128)(2,1)}, u32[]{:S(2)}, u32[]{:S(2)}) %collective-permute-start.17) | collective-permute-done | bytes 1048608 | tf_op jit(solution)/shard_map/ppermute | solution.py:481
  503.6 21.4 %collective-permute-done.18.refs_6_ = bf16[512,1024]{1,0:T(8,128)(2,1)} collective-permute-done((bf16[512,1024]{1,0:T(8,128)(2,1)}, bf16[512,1024]{1,0:T(8,128)(2,1)}, u32[]{:S(2)}, u32[]{:S(2)}) %collective-permute-start.18) | collective-permute-done | bytes 1048608 | tf_op jit(solution)/shard_map/ppermute | solution.py:481
  525.0 22.4 %collective-permute-done.19.refs_7_ = bf16[512,1024]{1,0:T(8,128)(2,1)} collective-permute-done((bf16[512,1024]{1,0:T(8,128)(2,1)}, bf16[512,1024]{1,0:T(8,128)(2,1)}, u32[]{:S(2)}, u32[]{:S(2)}) %collective-permute-start.19) | collective-permute-done | bytes 1048608 | tf_op jit(solution)/shard_map/ppermute | solution.py:481
  578.5 24.5 %collective-permute-done.20.refs_2_ = bf16[512,2048]{1,0:T(8,128)(2,1)} collective-permute-done((bf16[512,2048]{1,0:T(8,128)(2,1)}, bf16[512,2048]{1,0:T(8,128)(2,1)}, u32[]{:S(2)}, u32[]{:S(2)}) %collective-permute-start.20) | collective-permute-done | bytes 2097184 | tf_op jit(solution)/shard_map/ppermute | solution.py:481
  605.2 102.4 %collective-permute-done.23.refs_5_ = bf16[3,512,512]{2,1,0:T(8,128)(2,1)} collective-permute-done((bf16[3,512,512]{2,1,0:T(8,128)(2,1)}, bf16[3,512,512]{2,1,0:T(8,128)(2,1)}, u32[]{:S(2)}, u32[]{:S(2)}) %collective-permute-start.23) | collective-permute-done | bytes 1572896 | tf_op jit(solution)/shard_map/ppermute | solution.py:481
  723.0 23.3 %attn.6.refs_0_ = bf16[8,512,256]{2,1,0:T(8,128)(2,1)} custom-call(s32[3]{0:T(128)} %pad_add_fusion.idx_ref, s32[1]{0:T(128)} %bitcast.5.len_ref, bf16[4,512,512]{2,1,0:T(8,128)(2,1)} %get-tuple-element.343.refs_0_.refs_1_, bf16[4,512,512]{2,1,0:T(8,128)(2,1)} %get-tuple-element.343.refs_0_.refs_1_, bf16[4,512,512]{2,1,0:T(8,128)(2,1)} %get-tuple-element.344.refs_2_.refs_3_, ...), custom_call_target="tpu_custom_call" | custom-call | flops 6871947776 | bytes 6291456 | tf_op jit(solution)/shard_map/attn/pallas_call | solution.py:363
  753.0 32.4 %proj_gated.12.refs_1_ = bf16[4,512,1536]{2,1,0:T(8,128)(2,1)} custom-call(bf16[512,2048]{1,0:T(8,128)(2,1)} %get-tuple-element.366.refs_0_, bf16[512,2048]{1,0:T(8,128)(2,1)} %collective-permute-done.21.refs_1_, bf16[512,2048]{1,0:T(8,128)(2,1)} %collective-permute-done.20.refs_2_, bf16[512,2048]{1,0:T(8,128)(2,1)} %collective-permute-done.22.refs_3_, ...), custom_call_target="tpu_custom_call" | custom-call | flops 25769803776 | bytes 27262976 | tf_op jit(solution)/shard_map/proj_gated/pallas_call | solution.py:272
  837.9 23.0 %proj_gated.14.refs_1_ = bf16[2,512,2048]{2,1,0:T(8,128)(2,1)} custom-call(bf16[512,2048]{1,0:T(8,128)(2,1)} %get-tuple-element.385.refs_0_, bf16[512,2048]{1,0:T(8,128)(2,1)} %collective-permute-done.32.refs_1_, bf16[4,512,1024]{2,1,0:T(8,128)(2,1)} %bitcast.17, bf16[3,512,1024]{2,1,0:T(8,128)(2,1)} %collective-permute-done.24.refs_5_.refs_3_, ...), custom_call_target="tpu_custom_call" | custom-call | flops 17179869184 | bytes 25165824 | tf_op jit(solution)/shard_map/proj_gated/pallas_call | solution.py:272
  900.5 23.2 %attn.7.refs_0_ = bf16[8,512,256]{2,1,0:T(8,128)(2,1)} custom-call(s32[3]{0:T(128)} %pad_add_fusion.idx_ref, s32[1]{0:T(128)} %bitcast.6.len_ref, bf16[4,512,512]{2,1,0:T(8,128)(2,1)} %get-tuple-element.390.refs_0_.refs_1_, bf16[4,512,512]{2,1,0:T(8,128)(2,1)} %get-tuple-element.390.refs_0_.refs_1_, bf16[4,512,512]{2,1,0:T(8,128)(2,1)} %get-tuple-element.391.refs_2_.refs_3_, ...), custom_call_target="tpu_custom_call" | custom-call | flops 6871947776 | bytes 6291456 | tf_op jit(solution)/shard_map/attn/pallas_call | solution.py:363
  944.3 23.0 %proj_gated.15.refs_2_ = bf16[2,512,2048]{2,1,0:T(8,128)(2,1)} custom-call(bf16[512,2048]{1,0:T(8,128)(2,1)} %collective-permute-done.34.refs_2_.refs_0_, bf16[512,2048]{1,0:T(8,128)(2,1)} %collective-permute-done.35.refs_3_.refs_1_, bf16[4,512,1024]{2,1,0:T(8,128)(2,1)} %bitcast.18, bf16[3,512,1024]{2,1,0:T(8,128)(2,1)} %collective-permute-done.24.refs_5_.refs_3_, ...), custom_call_target="tpu_custom_call" | custom-call | flops 17179869184 | bytes 25165824 | tf_op jit(solution)/shard_map/proj_gated/pallas_call | solution.py:272
  1010.8 21.4 %collective-permute-done.48.refs_7_ = bf16[512,1024]{1,0:T(8,128)(2,1)} collective-permute-done((bf16[512,1024]{1,0:T(8,128)(2,1)}, bf16[512,1024]{1,0:T(8,128)(2,1)}, u32[]{:S(2)}, u32[]{:S(2)}) %collective-permute-start.48) | collective-permute-done | bytes 1048608 | tf_op jit(solution)/shard_map/ppermute | solution.py:481
  1055.7 22.5 %collective-permute-done.40.refs_5_ = bf16[512,1024]{1,0:T(8,128)(2,1)} collective-permute-done((bf16[512,1024]{1,0:T(8,128)(2,1)}, bf16[512,1024]{1,0:T(8,128)(2,1)}, u32[]{:S(2)}, u32[]{:S(2)}) %collective-permute-start.40) | collective-permute-done | bytes 1048608 | tf_op jit(solution)/shard_map/ppermute | solution.py:481
  1078.2 21.4 %collective-permute-done.41.refs_6_ = bf16[512,1024]{1,0:T(8,128)(2,1)} collective-permute-done((bf16[512,1024]{1,0:T(8,128)(2,1)}, bf16[512,1024]{1,0:T(8,128)(2,1)}, u32[]{:S(2)}, u32[]{:S(2)}) %collective-permute-start.41) | collective-permute-done | bytes 1048608 | tf_op jit(solution)/shard_map/ppermute | solution.py:481
  1099.6 21.7 %collective-permute-done.42.refs_7_ = bf16[512,1024]{1,0:T(8,128)(2,1)} collective-permute-done((bf16[512,1024]{1,0:T(8,128)(2,1)}, bf16[512,1024]{1,0:T(8,128)(2,1)}, u32[]{:S(2)}, u32[]{:S(2)}) %collective-permute-start.42) | collective-permute-done | bytes 1048608 | tf_op jit(solution)/shard_map/ppermute | solution.py:481
  (165 shorter events, 453.3 us)
Async XLA Ops:
  6.5 83.9 %all-gather.21.cloned.1.call-start = ((), (), s32[]{:S(2)}) async-start(), calls=%async_computation | async-start | bytes 2621440 | tf_op jit(solution)/shard_map/all_gather | solution.py:553
  9.8 183.2 %all-gather.23.cloned.1.call-start = ((), (), s32[]{:S(2)}) async-start(), calls=%async_computation.1 | async-start | bytes 5242880 | tf_op jit(solution)/shard_map/all_gather | solution.py:553
  29.0 250.1 %all-gather.25.cloned.1.call-start = ((), (), s32[]{:S(2)}) async-start(), calls=%async_computation.2 | async-start | bytes 5242880 | tf_op jit(solution)/shard_map/all_gather | solution.py:553
  31.9 297.7 %all-gather.27.cloned.1.call-start = ((), (), s32[]{:S(2)}) async-start(), calls=%async_computation.3 | async-start | bytes 3276800 | tf_op jit(solution)/shard_map/all_gather | solution.py:553
  34.6 343.6 %all-gather.29.cloned.1.call-start = ((), (), s32[]{:S(2)}) async-start(), calls=%async_computation.4 | async-start | bytes 3276800 | tf_op jit(solution)/shard_map/all_gather | solution.py:553
  37.3 377.1 %all-gather.31.cloned.1.call-start = ((), (), s32[]{:S(2)}) async-start(), calls=%async_computation.5 | async-start | bytes 2621440 | tf_op jit(solution)/shard_map/all_gather | solution.py:553
  39.9 516.6 %all-gather.33.cloned.1.call-start = ((), (), s32[]{:S(2)}) async-start(), calls=%async_computation.6 | async-start | bytes 5242880 | tf_op jit(solution)/shard_map/all_gather | solution.py:553
  44.3 702.1 %all-gather.35.cloned.1.call-start = ((), (), s32[]{:S(2)}) async-start(), calls=%async_computation.7 | async-start | bytes 5242880 | tf_op jit(solution)/shard_map/all_gather | solution.py:553
  90.2 93.7 %collective-permute-start.8 = (bf16[512,2048]{1,0:T(8,128)(2,1)}, bf16[512,2048]{1,0:T(8,128)(2,1)}, u32[]{:S(2)}, u32[]{:S(2)}) collective-permute-start(bf16[512,2048]{1,0:T(8,128)(2,1)} %ln.3.refs_0_.refs_4_), channel_id=1, source_target_pairs={{0,1},{1,0},{2,3},{3,2},{4,5},{5,4},{6,7},{7,6},{8,9},{9,8},{10,11... | collective-permute-start | bytes 6291464 | tf_op jit(solution)/shard_map/ppermute | solution.py:481
  139.1 669.8 %all-gather.37.cloned.1.call-start = ((), (), s32[]{:S(2)}) async-start(), calls=%async_computation.8 | async-start | bytes 3276800 | tf_op jit(solution)/shard_map/all_gather | solution.py:553
  198.3 86.0 %collective-permute-start.10 = (bf16[3,512,1024]{2,1,0:T(8,128)(2,1)}, bf16[3,512,1024]{2,1,0:T(8,128)(2,1)}, u32[]{:S(2)}, u32[]{:S(2)}) collective-permute-start(bf16[3,512,1024]{2,1,0:T(8,128)(2,1)} %pick.11), channel_id=1, source_target_pairs={{0,16},{16,0},{1,17},{17,1},{2,18},{18,2},{3,19},{19,3},{4,20},{20... | collective-permute-start | bytes 9437192 | tf_op jit(solution)/shard_map/ppermute | solution.py:481
  457.7 89.7 %collective-permute-start.19 = (bf16[512,1024]{1,0:T(8,128)(2,1)}, bf16[512,1024]{1,0:T(8,128)(2,1)}, u32[]{:S(2)}, u32[]{:S(2)}) collective-permute-start(bf16[512,1024]{1,0:T(8,128)(2,1)} %get-tuple-element.322), channel_id=1, source_target_pairs={{0,3},{1,2},{2,1},{3,0},{4,7},{5,6},{6,5},{7,4},{8,11},{9,10},{10,... | collective-permute-start | bytes 3145736 | tf_op jit(solution)/shard_map/ppermute | solution.py:481
  556.3 304.7 %all-gather.39.cloned.1.call-start = ((), (), s32[]{:S(2)}) async-start(), calls=%async_computation.9 | async-start | bytes 3276800 | tf_op jit(solution)/shard_map/all_gather | solution.py:553
  556.3 152.7 %collective-permute-start.21 = (bf16[512,2048]{1,0:T(8,128)(2,1)}, bf16[512,2048]{1,0:T(8,128)(2,1)}, u32[]{:S(2)}, u32[]{:S(2)}) collective-permute-start(bf16[512,2048]{1,0:T(8,128)(2,1)} %get-tuple-element.366.refs_0_), channel_id=1, source_target_pairs={{0,1},{1,0},{2,3},{3,2},{4,5},{5,4},{6,7},{7,6},{8,9},{9,8},{10,11... | collective-permute-start | bytes 6291464 | tf_op jit(solution)/shard_map/ppermute | solution.py:481
  603.0 106.0 %collective-permute-start.22 = (bf16[512,2048]{1,0:T(8,128)(2,1)}, bf16[512,2048]{1,0:T(8,128)(2,1)}, u32[]{:S(2)}, u32[]{:S(2)}) collective-permute-start(bf16[512,2048]{1,0:T(8,128)(2,1)} %collective-permute-done.20.refs_2_), channel_id=1, source_target_pairs={{0,1},{1,0},{2,3},{3,2},{4,5},{5,4},{6,7},{7,6},{8,9},{9,8},{10,11... | collective-permute-start | bytes 6291464 | tf_op jit(solution)/shard_map/ppermute | solution.py:481
  603.0 149.9 %collective-permute-start.24 = (bf16[3,512,1024]{2,1,0:T(8,128)(2,1)}, bf16[3,512,1024]{2,1,0:T(8,128)(2,1)}, u32[]{:S(2)}, u32[]{:S(2)}) collective-permute-start(bf16[3,512,1024]{2,1,0:T(8,128)(2,1)} %pick.16), channel_id=1, source_target_pairs={{0,16},{16,0},{1,17},{17,1},{2,18},{18,2},{3,19},{19,3},{4,20},{20... | collective-permute-start | bytes 9437192 | tf_op jit(solution)/shard_map/ppermute | solution.py:481
  603.3 104.2 %collective-permute-start.23 = (bf16[3,512,512]{2,1,0:T(8,128)(2,1)}, bf16[3,512,512]{2,1,0:T(8,128)(2,1)}, u32[]{:S(2)}, u32[]{:S(2)}) collective-permute-start(bf16[3,512,512]{2,1,0:T(8,128)(2,1)} %pick.15), channel_id=1, source_target_pairs={{0,16},{16,0},{1,17},{17,1},{2,18},{18,2},{3,19},{19,3},{4,20},{20... | collective-permute-start | bytes 4718600 | tf_op jit(solution)/shard_map/ppermute | solution.py:481
  605.1 146.4 %collective-permute-start.25 = (bf16[512,1024]{1,0:T(8,128)(2,1)}, bf16[512,1024]{1,0:T(8,128)(2,1)}, u32[]{:S(2)}, u32[]{:S(2)}) collective-permute-start(bf16[512,1024]{1,0:T(8,128)(2,1)} %get-tuple-element.353), channel_id=1, source_target_pairs={{0,1},{1,0},{2,3},{3,2},{4,5},{5,4},{6,7},{7,6},{8,9},{9,8},{10,11... | collective-permute-start | bytes 3145736 | tf_op jit(solution)/shard_map/ppermute | solution.py:481
  709.0 76.4 %collective-permute-start.26 = (bf16[512,1024]{1,0:T(8,128)(2,1)}, bf16[512,1024]{1,0:T(8,128)(2,1)}, u32[]{:S(2)}, u32[]{:S(2)}) collective-permute-start(bf16[512,1024]{1,0:T(8,128)(2,1)} %get-tuple-element.354), channel_id=1, source_target_pairs={{0,1},{1,0},{2,3},{3,2},{4,5},{5,4},{6,7},{7,6},{8,9},{9,8},{10,11... | collective-permute-start | bytes 3145736 | tf_op jit(solution)/shard_map/ppermute | solution.py:481
  882.8 101.6 %collective-permute-start.43 = (bf16[512,1024]{1,0:T(8,128)(2,1)}, bf16[512,1024]{1,0:T(8,128)(2,1)}, u32[]{:S(2)}, u32[]{:S(2)}) collective-permute-start(bf16[512,1024]{1,0:T(8,128)(2,1)} %get-tuple-element.427), channel_id=1, source_target_pairs={{0,1},{1,0},{2,3},{3,2},{4,5},{5,4},{6,7},{7,6},{8,9},{9,8},{10,11... | collective-permute-start | bytes 3145736 | tf_op jit(solution)/shard_map/ppermute | solution.py:481
  882.9 103.0 %collective-permute-start.45 = (bf16[512,1024]{1,0:T(8,128)(2,1)}, bf16[512,1024]{1,0:T(8,128)(2,1)}, u32[]{:S(2)}, u32[]{:S(2)}) collective-permute-start(bf16[512,1024]{1,0:T(8,128)(2,1)} %get-tuple-element.429), channel_id=1, source_target_pairs={{0,2},{1,3},{2,0},{3,1},{4,6},{5,7},{6,4},{7,5},{8,10},{9,11},{10,... | collective-permute-start | bytes 3145736 | tf_op jit(solution)/shard_map/ppermute | solution.py:481
  884.4 117.8 %collective-permute-start.47 = (bf16[512,1024]{1,0:T(8,128)(2,1)}, bf16[512,1024]{1,0:T(8,128)(2,1)}, u32[]{:S(2)}, u32[]{:S(2)}) collective-permute-start(bf16[512,1024]{1,0:T(8,128)(2,1)} %get-tuple-element.431), channel_id=1, source_target_pairs={{0,3},{1,2},{2,1},{3,0},{4,7},{5,6},{6,5},{7,4},{8,11},{9,10},{10,... | collective-permute-start | bytes 3145736 | tf_op jit(solution)/shard_map/ppermute | solution.py:481
  1010.8 88.9 %collective-permute-start.41 = (bf16[512,1024]{1,0:T(8,128)(2,1)}, bf16[512,1024]{1,0:T(8,128)(2,1)}, u32[]{:S(2)}, u32[]{:S(2)}) collective-permute-start(bf16[512,1024]{1,0:T(8,128)(2,1)} %get-tuple-element.422), channel_id=1, source_target_pairs={{0,3},{1,2},{2,1},{3,0},{4,7},{5,6},{6,5},{7,4},{8,11},{9,10},{10,... | collective-permute-start | bytes 3145736 | tf_op jit(solution)/shard_map/ppermute | solution.py:481
  1032.2 89.1 %collective-permute-start.42 = (bf16[512,1024]{1,0:T(8,128)(2,1)}, bf16[512,1024]{1,0:T(8,128)(2,1)}, u32[]{:S(2)}, u32[]{:S(2)}) collective-permute-start(bf16[512,1024]{1,0:T(8,128)(2,1)} %get-tuple-element.423), channel_id=1, source_target_pairs={{0,3},{1,2},{2,1},{3,0},{4,7},{5,6},{6,5},{7,4},{8,11},{9,10},{10,... | collective-permute-start | bytes 3145736 | tf_op jit(solution)/shard_map/ppermute | solution.py:481
  (37 other events, 1497.0 us)
Sparse Core Ops, SparseCore 0:
  10.0 45.4 all-gather.20
  57.1 78.1 all-gather.22
  136.9 79.2 all-gather.24
  217.5 54.1 all-gather.26
  273.2 53.5 all-gather.28
  328.2 44.7 all-gather.30
  374.6 78.1 all-gather.32
  454.4 79.2 all-gather.34
  556.4 50.9 all-gather.36
  608.8 53.5 all-gather.38
